TPU v7x, 32 devices: a whole 2x2x4 slice. The times are simulated.
32 devices in a mesh: grid: 8 (over z, y), band: 4 (over x, core).
Axes of the slice: x: 2, y: 2, z: 4, core: 2. Of those that a mesh axis runs over, the one named last changes fastest.
Arguments:
- orbitals: float32 [32, 16, 16, 512], P('grid', None, None, 'band'), may hold values from -80 to 80
- projectors: float32 [32, 16, 16, 512], P('grid', None, None, 'band'), may hold values from -0.09375 to 0.09375
- potential: float32 [32, 16, 16], P('grid'), may hold values from 0.3 to 3
Outputs:
- updated_orbitals: float32 [32, 16, 16, 512], P('grid', None, None, 'band')
- rayleigh_quotients: float32 [3, 512], P(None, 'band')
- residual_norms: float32 [3, 512], P(None, 'band')
All inputs are finite; a program needn't handle non-finite values.
Results may differ from a plain program's by a relative error of at most 0.00012.
Values sent between devices are 32-bit elements; how exact they have to be, the bound alone decides.
A program may use at most 128 MiB of HBM per device.

v0:
```python
import jax
import jax.numpy as jnp
from jax import lax
from jax.sharding import PartitionSpec as P

ITERS = 3
STENCIL = (-205.0 / 72.0, 8.0 / 5.0, -1.0 / 5.0, 8.0 / 315.0, -1.0 / 560.0)
STEP_LENGTH = 0.25
NORM_EPS = 1e-06
HIGHEST = lax.Precision.HIGHEST


def with_halo(block, sides, width):
    for axis, dim in sides:
        count = lax.axis_size(axis)
        forward = [(i, i + 1) for i in range(count - 1)]
        forward.append((count - 1, 0))
        backward = [(target, source) for source, target in forward]
        low = lax.ppermute(
            lax.slice_in_dim(block, block.shape[dim] - width, None, axis=dim), axis, forward
        )
        high = lax.ppermute(lax.slice_in_dim(block, 0, width, axis=dim), axis, backward)
        block = jnp.concatenate([low, block, high], axis=dim)
    return block


def matmul(left, right):
    return jnp.dot(left, right, precision=HIGHEST, preferred_element_type=jnp.float32)


def laplacian(grid_field):
    padded = with_halo(grid_field, (("grid", 0),), 4)
    planes_here = grid_field.shape[0]
    result = 3.0 * STENCIL[0] * grid_field
    for distance in range(1, 5):
        result = result + STENCIL[distance] * (
            padded[4 + distance : 4 + distance + planes_here]
            + padded[4 - distance : 4 - distance + planes_here]
        )
    for dimension in (1, 2):
        for distance in range(1, 5):
            result = result + STENCIL[distance] * (
                jnp.roll(grid_field, distance, dimension)
                + jnp.roll(grid_field, -distance, dimension)
            )
    return result


def local(orbitals, projectors, potential):
    grid_shape = orbitals.shape
    local_bands = orbitals.shape[3]
    total_bands = local_bands * lax.axis_size("band")
    first_band = lax.axis_index("band") * local_bands
    vectors = orbitals.reshape(-1, local_bands)
    every_projector = lax.all_gather(projectors, "band", axis=3, tiled=True).reshape(
        -1, projectors.shape[3] * lax.axis_size("band")
    )
    identity_matrix = jnp.eye(total_bands, dtype=jnp.float32)
    quotient_list = []
    norm_list = []
    for iteration in range(ITERS):
        gathered = lax.all_gather(vectors.reshape(grid_shape), "band", axis=3, tiled=True).reshape(
            -1, total_bands
        )
        margin = lax.psum(matmul(gathered.T, gathered), "grid")
        factor = jnp.linalg.cholesky(margin)
        inverse = jax.scipy.linalg.solve_triangular(factor, identity_matrix, lower=True)
        transform = inverse.T
        vectors = matmul(gathered, lax.dynamic_slice_in_dim(transform, first_band, local_bands, 1))
        coupling = lax.psum(matmul(every_projector.T, vectors), "grid")
        exchange_part = matmul(every_projector, coupling)
        grid_field = vectors.reshape(grid_shape)
        applied = (-0.5 * laplacian(grid_field) + potential[..., None] * grid_field).reshape(
            -1, local_bands
        ) - exchange_part
        rayleigh = lax.psum(jnp.sum(vectors * applied, axis=0), "grid")
        residual = applied - rayleigh[None, :] * vectors
        squared = lax.psum(jnp.sum(residual * residual, axis=0), "grid")
        vectors = vectors - STEP_LENGTH * residual / jnp.sqrt(squared + NORM_EPS)[None, :]
        quotient_list.append(rayleigh)
        norm_list.append(jnp.sqrt(squared))
    return (vectors.reshape(grid_shape), jnp.stack(quotient_list), jnp.stack(norm_list))


def solution(mesh):
    return jax.shard_map(
        local,
        mesh=mesh,
        in_specs=(
            P("grid", None, None, "band"),
            P("grid", None, None, "band"),
            P("grid", None, None),
        ),
        out_specs=(P("grid", None, None, "band"), P(None, "band"), P(None, "band")),
        check_vma=False,
    )
```

profile of v0, /device:TPU:0, one launch (start us, length us, event | category | flops | bytes accessed | tf_op | source)
XLA Modules:
  0.0 1202.1 jit_solution(3516485684897773808)
XLA Ops:
  7.9 27.1 %all-gather.5.cloned.1.call-done = f32[4,16,16,512]{3,2,1,0:T(8,128)} async-done(((f32[4,16,16,128]{3,2,1,0:T(8,128)}), f32[4,16,16,512]{3,2,1,0:T(8,128)}) %all-gather.5.cloned.1.call-update) | async-done | bytes 2097168 | tf_op jit(solution)/shard_map/all_gather | solution.py:62
  43.0 77.3 %all-reduce.8.cloned.1.call-done = f32[512,512]{0,1:T(8,128)} async-done(((f32[512,512]{0,1:T(8,128)}), f32[512,512]{0,1:T(8,128)}) %all-reduce.8.cloned.1.call-update) | async-done | bytes 1048592 | tf_op jit(solution)/shard_map/psum | solution.py:65
  218.7 39.3 %custom-call.34 = f32[4,128,128]{1,2,0:T(8,128)S(1)} custom-call(f32[4,128,128]{2,1,0:T(8,128)S(1)} %get-tuple-element.25), custom_call_target="InvertDiagBlocksLowerTriangular" | custom-call | tf_op jit(solution)/shard_map/jit(_solve_triangular)/triangular_solve | solution.py:67
  296.4 58.0 %all-reduce.10.cloned.1.call-done = f32[512,128]{0,1:T(8,128)} async-done(((f32[512,128]{0,1:T(8,128)}), f32[512,128]{0,1:T(8,128)}) %all-reduce.10.cloned.1.call-update) | async-done | bytes 262160 | tf_op jit(solution)/shard_map/psum | solution.py:70
  357.9 19.6 %psum.86 = f32[128]{0:T(128)S(1)} all-reduce(f32[128]{0:T(128)S(1)} %get-tuple-element.195), channel_id=1, replica_groups=mesh['grid'=8,'band'=4] {'grid'}, use_global_device_ids=true, to_apply=%region_11.14 | all-reduce | flops 128 | bytes 1024 | tf_op jit(solution)/shard_map/psum | solution.py:76
  377.8 17.1 %psum.87 = f32[128]{0:T(128)S(1)} all-reduce(f32[128]{0:T(128)S(1)} %multiply_reduce_fusion.4), channel_id=1, replica_groups=mesh['grid'=8,'band'=4] {'grid'}, use_global_device_ids=true, to_apply=%region_13.16 | all-reduce | flops 128 | bytes 1024 | tf_op jit(solution)/shard_map/psum | solution.py:78
  398.0 21.6 %all-gather.9.cloned.1.call-done = f32[4,16,16,512]{3,2,1,0:T(8,128)} async-done(((f32[4,16,16,128]{3,2,1,0:T(8,128)}), f32[4,16,16,512]{3,2,1,0:T(8,128)}) %all-gather.9.cloned.1.call-update) | async-done | bytes 2097168 | tf_op jit(solution)/shard_map/all_gather | solution.py:62
  426.8 77.9 %all-reduce.12.cloned.1.call-done = f32[512,512]{0,1:T(8,128)} async-done(((f32[512,512]{0,1:T(8,128)}), f32[512,512]{0,1:T(8,128)}) %all-reduce.12.cloned.1.call-update) | async-done | bytes 1048592 | tf_op jit(solution)/shard_map/psum | solution.py:65
  584.6 11.7 cholesky.503
  602.6 11.8 while.7
  615.1 40.1 %custom-call.38 = f32[4,128,128]{1,2,0:T(8,128)S(1)} custom-call(f32[4,128,128]{2,1,0:T(8,128)} %copy-done.45), custom_call_target="InvertDiagBlocksLowerTriangular" | custom-call | tf_op jit(solution)/shard_map/jit(_solve_triangular)/triangular_solve | solution.py:67
  680.7 14.4 %collective-permute-done.2 = f32[4,16,16,128]{3,2,1,0:T(8,128)} collective-permute-done((f32[4,16,16,128]{3,2,1,0:T(8,128)S(1)}, f32[4,16,16,128]{3,2,1,0:T(8,128)}, u32[]{:S(2)}, u32[]{:S(2)}) %collective-permute-start.2) | collective-permute-done | bytes 524320 | tf_op jit(solution)/shard_map/ppermute | solution.py:22
  701.9 51.0 %all-reduce.14.cloned.1.call-done = f32[512,128]{0,1:T(8,128)} async-done(((f32[512,128]{0,1:T(8,128)}), f32[512,128]{0,1:T(8,128)}) %all-reduce.14.cloned.1.call-update) | async-done | bytes 262160 | tf_op jit(solution)/shard_map/psum | solution.py:70
  756.4 19.6 %psum.90 = f32[128]{0:T(128)S(1)} all-reduce(f32[128]{0:T(128)S(1)} %get-tuple-element.199), channel_id=1, replica_groups=mesh['grid'=8,'band'=4] {'grid'}, use_global_device_ids=true, to_apply=%region_17.20 | all-reduce | flops 128 | bytes 1024 | tf_op jit(solution)/shard_map/psum | solution.py:76
  776.2 17.1 %psum.91 = f32[128]{0:T(128)S(1)} all-reduce(f32[128]{0:T(128)S(1)} %multiply_reduce_fusion.2), channel_id=1, replica_groups=mesh['grid'=8,'band'=4] {'grid'}, use_global_device_ids=true, to_apply=%region_19.22 | all-reduce | flops 128 | bytes 1024 | tf_op jit(solution)/shard_map/psum | solution.py:78
  797.0 21.6 %all-gather.11.cloned.1.call-done = f32[4,16,16,512]{3,2,1,0:T(8,128)} async-done(((f32[4,16,16,128]{3,2,1,0:T(8,128)}), f32[4,16,16,512]{3,2,1,0:T(8,128)}) %all-gather.11.cloned.1.call-update) | async-done | bytes 2097168 | tf_op jit(solution)/shard_map/all_gather | solution.py:62
  825.5 78.3 %all-reduce.16.cloned.1.call-done = f32[512,512]{0,1:T(8,128)} async-done(((f32[512,512]{0,1:T(8,128)}), f32[512,512]{0,1:T(8,128)}) %all-reduce.16.cloned.1.call-update) | async-done | bytes 1048592 | tf_op jit(solution)/shard_map/psum | solution.py:65
  983.7 11.7 cholesky.575
  1001.9 11.8 while.8
  1014.4 40.1 %custom-call.42 = f32[4,128,128]{1,2,0:T(8,128)S(1)} custom-call(f32[4,128,128]{2,1,0:T(8,128)} %copy-done.44), custom_call_target="InvertDiagBlocksLowerTriangular" | custom-call | tf_op jit(solution)/shard_map/jit(_solve_triangular)/triangular_solve | solution.py:67
  1079.6 14.8 %collective-permute-done.4 = f32[4,16,16,128]{3,2,1,0:T(8,128)} collective-permute-done((f32[4,16,16,128]{3,2,1,0:T(8,128)S(1)}, f32[4,16,16,128]{3,2,1,0:T(8,128)}, u32[]{:S(2)}, u32[]{:S(2)}) %collective-permute-start.4) | collective-permute-done | bytes 524320 | tf_op jit(solution)/shard_map/ppermute | solution.py:22
  1101.2 51.0 %all-reduce.18.cloned.1.call-done = f32[512,128]{0,1:T(8,128)} async-done(((f32[512,128]{0,1:T(8,128)}), f32[512,128]{0,1:T(8,128)}) %all-reduce.18.cloned.1.call-update) | async-done | bytes 262160 | tf_op jit(solution)/shard_map/psum | solution.py:70
  1155.7 19.6 %psum.94 = f32[128]{0:T(128)S(1)} all-reduce(f32[128]{0:T(128)S(1)} %get-tuple-element.203), channel_id=1, replica_groups=mesh['grid'=8,'band'=4] {'grid'}, use_global_device_ids=true, to_apply=%region_23.26 | all-reduce | flops 128 | bytes 1024 | tf_op jit(solution)/shard_map/psum | solution.py:76
  1175.5 17.1 %psum.95 = f32[128]{0:T(128)S(1)} all-reduce(f32[128]{0:T(128)S(1)} %multiply_reduce_fusion), channel_id=1, replica_groups=mesh['grid'=8,'band'=4] {'grid'}, use_global_device_ids=true, to_apply=%region_25.28 | all-reduce | flops 128 | bytes 1024 | tf_op jit(solution)/shard_map/psum | solution.py:78
  (353 shorter events, 440.8 us)
Async XLA Ops:
  7.2 27.9 %all-gather.5.cloned.1.call-start = ((), (), s32[]{:S(2)}) async-start(), calls=%async_computation | async-start | bytes 2621440 | tf_op jit(solution)/shard_map/all_gather | solution.py:62
  7.9 112.4 %all-reduce.8.cloned.1.call-start = ((), (), s32[]{:S(2)}) async-start(), calls=%async_computation.1 | async-start | bytes 2097152 | tf_op jit(solution)/shard_map/psum | solution.py:65
  41.8 236.4 %all-gather.7.cloned.1.call-start = ((), (), s32[]{:S(2)}) async-start(), calls=%async_computation.2 | async-start | bytes 2621440 | tf_op jit(solution)/shard_map/all_gather | solution.py:55
  42.5 311.9 %all-reduce.10.cloned.1.call-start = ((), (), s32[]{:S(2)}) async-start(), calls=%async_computation.3 | async-start | bytes 524288 | tf_op jit(solution)/shard_map/psum | solution.py:70
  43.0 217.1 %copy-start.4 = (f32[512,512]{1,0:T(8,128)}, f32[512,512]{1,0:T(8,128)S(1)}, u32[]{:S(2)}) copy-start(f32[512,512]{1,0:T(8,128)S(1)} %fusion.6) | copy-start | bytes 3145732
  263.7 24.9 %collective-permute-start = (f32[4,16,16,128]{3,2,1,0:T(8,128)S(1)}, f32[4,16,16,128]{3,2,1,0:T(8,128)S(1)}, u32[]{:S(2)}, u32[]{:S(2)}) collective-permute-start(f32[4,16,16,128]{3,2,1,0:T(8,128)S(1)} %bitcast.253), channel_id=1, source_target_pairs={{4,0},{8,4},{12,8},{16,12},{20,16},{24,20},{28,24},{0,28},{5,1},{9... | collective-permute-start | bytes 1572872 | tf_op jit(solution)/shard_map/ppermute | solution.py:22
  266.7 21.9 %collective-permute-start.1 = (f32[4,16,16,128]{3,2,1,0:T(8,128)S(1)}, f32[4,16,16,128]{3,2,1,0:T(8,128)S(1)}, u32[]{:S(2)}, u32[]{:S(2)}) collective-permute-start(f32[4,16,16,128]{3,2,1,0:T(8,128)S(1)} %bitcast.254), channel_id=1, source_target_pairs={{0,4},{4,8},{8,12},{12,16},{16,20},{20,24},{24,28},{28,0},{1,5},{5... | collective-permute-start | bytes 1572872 | tf_op jit(solution)/shard_map/ppermute | solution.py:19
  281.8 137.8 %all-gather.9.cloned.1.call-start = ((), (), s32[]{:S(2)}) async-start(), calls=%async_computation.4 | async-start | bytes 2621440 | tf_op jit(solution)/shard_map/all_gather | solution.py:62
  289.6 64.8 %copy-start = (f32[4,16,16,512]{3,2,1,0:T(8,128)S(1)}, f32[4,16,16,512]{3,2,1,0:T(8,128)}, u32[]{:S(2)}) copy-start(f32[4,16,16,512]{3,2,1,0:T(8,128)} %all-gather.7.cloned.1.call-done) | copy-start | bytes 6291460
  398.0 106.8 %all-reduce.12.cloned.1.call-start = ((), (), s32[]{:S(2)}) async-start(), calls=%async_computation.5 | async-start | bytes 2097152 | tf_op jit(solution)/shard_map/psum | solution.py:65
  426.3 326.6 %all-reduce.14.cloned.1.call-start = ((), (), s32[]{:S(2)}) async-start(), calls=%async_computation.6 | async-start | bytes 524288 | tf_op jit(solution)/shard_map/psum | solution.py:70
  559.6 95.7 %copy-start.5 = (f32[512,512]{1,0:T(8,128)S(1)}, f32[512,512]{1,0:T(8,128)}, u32[]{:S(2)}) copy-start(f32[512,512]{1,0:T(8,128)} %copy-done.4) | copy-start | bytes 3145732
  669.1 26.0 %collective-permute-start.2 = (f32[4,16,16,128]{3,2,1,0:T(8,128)S(1)}, f32[4,16,16,128]{3,2,1,0:T(8,128)}, u32[]{:S(2)}, u32[]{:S(2)}) collective-permute-start(f32[4,16,16,128]{3,2,1,0:T(8,128)S(1)} %bitcast.221), channel_id=1, source_target_pairs={{4,0},{8,4},{12,8},{16,12},{20,16},{24,20},{28,24},{0,28},{5,1},{9... | collective-permute-start | bytes 1572872 | tf_op jit(solution)/shard_map/ppermute | solution.py:22
  672.0 23.1 %collective-permute-start.3 = (f32[4,16,16,128]{3,2,1,0:T(8,128)S(1)}, f32[4,16,16,128]{3,2,1,0:T(8,128)}, u32[]{:S(2)}, u32[]{:S(2)}) collective-permute-start(f32[4,16,16,128]{3,2,1,0:T(8,128)S(1)} %bitcast.222), channel_id=1, source_target_pairs={{0,4},{4,8},{8,12},{12,16},{16,20},{20,24},{24,28},{28,0},{1,5},{5... | collective-permute-start | bytes 1572872 | tf_op jit(solution)/shard_map/ppermute | solution.py:19
  680.0 138.6 %all-gather.11.cloned.1.call-start = ((), (), s32[]{:S(2)}) async-start(), calls=%async_computation.7 | async-start | bytes 2621440 | tf_op jit(solution)/shard_map/all_gather | solution.py:62
  796.9 106.8 %all-reduce.16.cloned.1.call-start = ((), (), s32[]{:S(2)}) async-start(), calls=%async_computation.8 | async-start | bytes 2097152 | tf_op jit(solution)/shard_map/psum | solution.py:65
  825.3 326.9 %all-reduce.18.cloned.1.call-start = ((), (), s32[]{:S(2)}) async-start(), calls=%async_computation.9 | async-start | bytes 524288 | tf_op jit(solution)/shard_map/psum | solution.py:70
  958.7 95.8 %copy-start.6 = (f32[512,512]{1,0:T(8,128)S(1)}, f32[512,512]{1,0:T(8,128)}, u32[]{:S(2)}) copy-start(f32[512,512]{1,0:T(8,128)} %copy-done.4) | copy-start | bytes 3145732
  1068.4 26.0 %collective-permute-start.4 = (f32[4,16,16,128]{3,2,1,0:T(8,128)S(1)}, f32[4,16,16,128]{3,2,1,0:T(8,128)}, u32[]{:S(2)}, u32[]{:S(2)}) collective-permute-start(f32[4,16,16,128]{3,2,1,0:T(8,128)S(1)} %bitcast.240), channel_id=1, source_target_pairs={{4,0},{8,4},{12,8},{16,12},{20,16},{24,20},{28,24},{0,28},{5,1},{9... | collective-permute-start | bytes 1572872 | tf_op jit(solution)/shard_map/ppermute | solution.py:22
  1071.3 23.1 %collective-permute-start.5 = (f32[4,16,16,128]{3,2,1,0:T(8,128)S(1)}, f32[4,16,16,128]{3,2,1,0:T(8,128)}, u32[]{:S(2)}, u32[]{:S(2)}) collective-permute-start(f32[4,16,16,128]{3,2,1,0:T(8,128)S(1)} %bitcast.241), channel_id=1, source_target_pairs={{0,4},{4,8},{8,12},{12,16},{16,20},{20,24},{24,28},{28,0},{1,5},{5... | collective-permute-start | bytes 1572872 | tf_op jit(solution)/shard_map/ppermute | solution.py:19
  1079.4 15.0 %copy-start.21 = (f32[4,16,15,128]{3,2,1,0:T(8,128)S(1)}, f32[4,16,15,128]{3,2,1,0:T(8,128)}, u32[]{:S(2)}) copy-start(f32[4,16,15,128]{3,2,1,0:T(8,128)} %get-tuple-element.79) | copy-start | bytes 1474564
  1079.4 15.0 %copy-start.22 = (f32[4,16,15,128]{3,2,1,0:T(8,128)S(1)}, f32[4,16,15,128]{3,2,1,0:T(8,128)}, u32[]{:S(2)}) copy-start(f32[4,16,15,128]{3,2,1,0:T(8,128)} %get-tuple-element.80) | copy-start | bytes 1474564
  1079.4 15.0 %copy-start.23 = (f32[4,16,14,128]{3,2,1,0:T(8,128)S(1)}, f32[4,16,14,128]{3,2,1,0:T(8,128)}, u32[]{:S(2)}) copy-start(f32[4,16,14,128]{3,2,1,0:T(8,128)} %get-tuple-element.83) | copy-start | bytes 1376260
  1155.7 38.2 %copy-start.46 = (f32[1,128]{1,0:T(1,128)S(1)}, f32[1,128]{1,0:T(1,128)}, u32[]{:S(2)}) copy-start(f32[1,128]{1,0:T(1,128)} %get-tuple-element.189) | copy-start | bytes 1540
  (39 other events, 315.3 us)
Sparse Core Ops, SparseCore 0:
  9.5 25.5 all-gather.4
  41.9 78.3 all-reduce.7
  121.8 22.4 all-gather.6
  282.0 72.4 all-reduce.9
  398.1 21.4 all-gather.8
  426.4 78.2 all-reduce.11
  680.1 72.7 all-reduce.13
  797.0 21.4 all-gather.10
  825.4 78.3 all-reduce.15
  1079.5 72.6 all-reduce.17
where the time goes:
time: 1210 us; the launch traced here: 1200 us
  waiting for transfers between devices  501 us (41%)
  other arithmetic  387 us (32%)
  blocking collectives  110 us (9%)
  local copies, waits for them, and re-layouts  93.1 us (8%)
  matrix products  77.4 us (6%)
  between operations  22.9 us (2%)
    another operation x44, other arithmetic, local(): factor = jnp.linalg.cholesky(margin)  240 us
    psum x3, waiting for transfers between devices, local(): margin = lax.psum(matmul(gathered.T, gathered), 'grid')  233 us
    psum x3, waiting for transfers between devices, local(): coupling = lax.psum(matmul(every_projector.T, vectors), 'grid')  160 us
    another operation x7, other arithmetic, local(): jax.scipy.linalg.solve_triangular(factor, identity_matrix, lower=True)  125 us
    all_gather x3, waiting for transfers between devices, local(): lax.all_gather(vectors.reshape(grid_shape), 'band', axis=3, tiled=True)  70.3 us
    psum x3, blocking collectives, local(): rayleigh = lax.psum(jnp.sum(vectors * applied, axis=0), 'grid')  58.9 us
    psum x3, blocking collectives, local(): squared = lax.psum(jnp.sum(residual * residual, axis=0), 'grid')  51.4 us
    dot_general x12, matrix products, matmul(): jnp.dot(left, right, precision=HIGHEST, preferred_element_type=jnp.float32)  44.3 us
  transfers between devices with their start and end apart: 16, of which 12 were waited for; matrix products, arithmetic and copies ran while one was open for 16% of the time, Pallas kernels for 0%

commit v1 on v0

--- a/solution.py
+++ b/solution.py
@@ -2,6 +2,7 @@
 import jax.numpy as jnp
 from jax import lax
 from jax.sharding import PartitionSpec as P
+from jax.lax import all_gather
 
 ITERS = 3
 STENCIL = (-205.0 / 72.0, 8.0 / 5.0, -1.0 / 5.0, 8.0 / 315.0, -1.0 / 560.0)
@@ -59,9 +60,8 @@
     quotient_list = []
     norm_list = []
     for iteration in range(ITERS):
-        gathered = lax.all_gather(vectors.reshape(grid_shape), "band", axis=3, tiled=True).reshape(
-            -1, total_bands
-        )
+        refer_masks = lambda inp: jnp.concatenate(all_gather(inp, axis_name="band"), axis=3)
+        gathered = refer_masks(vectors.reshape(grid_shape)).reshape(-1, total_bands)
         margin = lax.psum(matmul(gathered.T, gathered), "grid")
         factor = jnp.linalg.cholesky(margin)
         inverse = jax.scipy.linalg.solve_triangular(factor, identity_matrix, lower=True)

time: 1210 us -> 1220 us (level)
  local copies, waits for them, and re-layouts: 93.1 us -> 107 us
where the time goes in v1:
time: 1220 us; the launch traced here: 1210 us
  waiting for transfers between devices  500 us (41%)
  other arithmetic  387 us (32%)
  blocking collectives  110 us (9%)
  local copies, waits for them, and re-layouts  107 us (9%)
  matrix products  70.8 us (6%)
  between operations  23.6 us (2%)
    another operation x44, other arithmetic, local(): factor = jnp.linalg.cholesky(margin)  240 us
    psum x3, waiting for transfers between devices, local(): margin = lax.psum(matmul(gathered.T, gathered), 'grid')  233 us
    psum x3, waiting for transfers between devices, local(): coupling = lax.psum(matmul(every_projector.T, vectors), 'grid')  160 us
    another operation x7, other arithmetic, local(): jax.scipy.linalg.solve_triangular(factor, identity_matrix, lower=True)  125 us
    all_gather x3, waiting for transfers between devices, local(): all_gather(inp, axis_name='band')  69.6 us
    psum x3, blocking collectives, local(): rayleigh = lax.psum(jnp.sum(vectors * applied, axis=0), 'grid')  58.9 us
    psum x3, blocking collectives, local(): squared = lax.psum(jnp.sum(residual * residual, axis=0), 'grid')  51.4 us
    dot_general x12, matrix products, matmul(): jnp.dot(left, right, precision=HIGHEST, preferred_element_type=jnp.float32)  37.8 us
  transfers between devices with their start and end apart: 16, of which 12 were waited for; matrix products, arithmetic and copies ran while one was open for 16% of the time, Pallas kernels for 0%

profile of v1, /device:TPU:0, one launch (start us, length us, event | category | flops | bytes accessed | tf_op | source)
XLA Modules:
  0.0 1209.1 jit_solution(1648069849725123500)
XLA Ops:
  7.9 26.9 %all-gather.12.cloned.1.call-done = f32[16,16,16,128]{3,2,1,0:T(8,128)} async-done(((f32[4,16,16,128]{3,2,1,0:T(8,128)}), f32[16,16,16,128]{3,2,1,0:T(8,128)}) %all-gather.12.cloned.1.call-update) | async-done | bytes 2097168 | tf_op jit(solution)/shard_map/all_gather | solution.py:63
  44.9 77.2 %all-reduce.8.cloned.1.call-done = f32[512,512]{0,1:T(8,128)} async-done(((f32[512,512]{0,1:T(8,128)}), f32[512,512]{0,1:T(8,128)}) %all-reduce.8.cloned.1.call-update) | async-done | bytes 1048592 | tf_op jit(solution)/shard_map/psum | solution.py:65
  220.6 39.3 %custom-call.34 = f32[4,128,128]{1,2,0:T(8,128)S(1)} custom-call(f32[4,128,128]{2,1,0:T(8,128)S(1)} %get-tuple-element.25), custom_call_target="InvertDiagBlocksLowerTriangular" | custom-call | tf_op jit(solution)/shard_map/jit(_solve_triangular)/triangular_solve | solution.py:67
  298.3 58.0 %all-reduce.10.cloned.1.call-done = f32[512,128]{0,1:T(8,128)} async-done(((f32[512,128]{0,1:T(8,128)}), f32[512,128]{0,1:T(8,128)}) %all-reduce.10.cloned.1.call-update) | async-done | bytes 262160 | tf_op jit(solution)/shard_map/psum | solution.py:70
  359.8 19.6 %psum.86 = f32[128]{0:T(128)S(1)} all-reduce(f32[128]{0:T(128)S(1)} %get-tuple-element.195), channel_id=1, replica_groups=mesh['grid'=8,'band'=4] {'grid'}, use_global_device_ids=true, to_apply=%region_11.14 | all-reduce | flops 128 | bytes 1024 | tf_op jit(solution)/shard_map/psum | solution.py:76
  379.7 17.1 %psum.87 = f32[128]{0:T(128)S(1)} all-reduce(f32[128]{0:T(128)S(1)} %multiply_reduce_fusion.4), channel_id=1, replica_groups=mesh['grid'=8,'band'=4] {'grid'}, use_global_device_ids=true, to_apply=%region_13.16 | all-reduce | flops 128 | bytes 1024 | tf_op jit(solution)/shard_map/psum | solution.py:78
  399.9 21.3 %all-gather.8.cloned.1.call-done = f32[4,4,16,16,128]{4,3,2,1,0:T(8,128)} async-done(((f32[1,4,16,16,128]{4,3,2,1,0:T(8,128)}), f32[4,4,16,16,128]{4,3,2,1,0:T(8,128)}) %all-gather.8.cloned.1.call-update) | async-done | bytes 2097168 | tf_op jit(solution)/shard_map/all_gather | solution.py:63
  430.5 78.0 %all-reduce.12.cloned.1.call-done = f32[512,512]{0,1:T(8,128)} async-done(((f32[512,512]{0,1:T(8,128)}), f32[512,512]{0,1:T(8,128)}) %all-reduce.12.cloned.1.call-update) | async-done | bytes 1048592 | tf_op jit(solution)/shard_map/psum | solution.py:65
  588.5 11.7 cholesky.503
  606.8 12.0 while.7
  619.5 40.1 %custom-call.38 = f32[4,128,128]{1,2,0:T(8,128)S(1)} custom-call(f32[4,128,128]{2,1,0:T(8,128)} %copy-done.48), custom_call_target="InvertDiagBlocksLowerTriangular" | custom-call | tf_op jit(solution)/shard_map/jit(_solve_triangular)/triangular_solve | solution.py:67
  685.2 14.3 %collective-permute-done.2 = f32[4,16,16,128]{3,2,1,0:T(8,128)} collective-permute-done((f32[4,16,16,128]{3,2,1,0:T(8,128)S(1)}, f32[4,16,16,128]{3,2,1,0:T(8,128)}, u32[]{:S(2)}, u32[]{:S(2)}) %collective-permute-start.2) | collective-permute-done | bytes 524320 | tf_op jit(solution)/shard_map/ppermute | solution.py:23
  706.3 51.0 %all-reduce.14.cloned.1.call-done = f32[512,128]{0,1:T(8,128)} async-done(((f32[512,128]{0,1:T(8,128)}), f32[512,128]{0,1:T(8,128)}) %all-reduce.14.cloned.1.call-update) | async-done | bytes 262160 | tf_op jit(solution)/shard_map/psum | solution.py:70
  760.9 19.6 %psum.90 = f32[128]{0:T(128)S(1)} all-reduce(f32[128]{0:T(128)S(1)} %get-tuple-element.199), channel_id=1, replica_groups=mesh['grid'=8,'band'=4] {'grid'}, use_global_device_ids=true, to_apply=%region_17.20 | all-reduce | flops 128 | bytes 1024 | tf_op jit(solution)/shard_map/psum | solution.py:76
  780.7 17.1 %psum.91 = f32[128]{0:T(128)S(1)} all-reduce(f32[128]{0:T(128)S(1)} %multiply_reduce_fusion.2), channel_id=1, replica_groups=mesh['grid'=8,'band'=4] {'grid'}, use_global_device_ids=true, to_apply=%region_19.22 | all-reduce | flops 128 | bytes 1024 | tf_op jit(solution)/shard_map/psum | solution.py:78
  801.4 21.3 %all-gather.10.cloned.1.call-done = f32[4,4,16,16,128]{4,3,2,1,0:T(8,128)} async-done(((f32[1,4,16,16,128]{4,3,2,1,0:T(8,128)}), f32[4,4,16,16,128]{4,3,2,1,0:T(8,128)}) %all-gather.10.cloned.1.call-update) | async-done | bytes 2097168 | tf_op jit(solution)/shard_map/all_gather | solution.py:63
  831.8 78.2 %all-reduce.16.cloned.1.call-done = f32[512,512]{0,1:T(8,128)} async-done(((f32[512,512]{0,1:T(8,128)}), f32[512,512]{0,1:T(8,128)}) %all-reduce.16.cloned.1.call-update) | async-done | bytes 1048592 | tf_op jit(solution)/shard_map/psum | solution.py:65
  990.1 11.7 cholesky.575
  1008.6 12.0 while.8
  1021.3 40.1 %custom-call.42 = f32[4,128,128]{1,2,0:T(8,128)S(1)} custom-call(f32[4,128,128]{2,1,0:T(8,128)} %copy-done.47), custom_call_target="InvertDiagBlocksLowerTriangular" | custom-call | tf_op jit(solution)/shard_map/jit(_solve_triangular)/triangular_solve | solution.py:67
  1086.6 14.7 %collective-permute-done.4 = f32[4,16,16,128]{3,2,1,0:T(8,128)} collective-permute-done((f32[4,16,16,128]{3,2,1,0:T(8,128)S(1)}, f32[4,16,16,128]{3,2,1,0:T(8,128)}, u32[]{:S(2)}, u32[]{:S(2)}) %collective-permute-start.4) | collective-permute-done | bytes 524320 | tf_op jit(solution)/shard_map/ppermute | solution.py:23
  1108.1 51.1 %all-reduce.18.cloned.1.call-done = f32[512,128]{0,1:T(8,128)} async-done(((f32[512,128]{0,1:T(8,128)}), f32[512,128]{0,1:T(8,128)}) %all-reduce.18.cloned.1.call-update) | async-done | bytes 262160 | tf_op jit(solution)/shard_map/psum | solution.py:70
  1162.7 19.6 %psum.94 = f32[128]{0:T(128)S(1)} all-reduce(f32[128]{0:T(128)S(1)} %get-tuple-element.203), channel_id=1, replica_groups=mesh['grid'=8,'band'=4] {'grid'}, use_global_device_ids=true, to_apply=%region_23.26 | all-reduce | flops 128 | bytes 1024 | tf_op jit(solution)/shard_map/psum | solution.py:76
  1182.5 17.1 %psum.95 = f32[128]{0:T(128)S(1)} all-reduce(f32[128]{0:T(128)S(1)} %multiply_reduce_fusion), channel_id=1, replica_groups=mesh['grid'=8,'band'=4] {'grid'}, use_global_device_ids=true, to_apply=%region_25.28 | all-reduce | flops 128 | bytes 1024 | tf_op jit(solution)/shard_map/psum | solution.py:78
  (362 shorter events, 447.9 us)
Async XLA Ops:
  7.2 27.7 %all-gather.12.cloned.1.call-start = ((), (), s32[]{:S(2)}) async-start(), calls=%async_computation.9 | async-start | bytes 2621440 | tf_op jit(solution)/shard_map/all_gather | solution.py:63
  7.9 114.2 %all-reduce.8.cloned.1.call-start = ((), (), s32[]{:S(2)}) async-start(), calls=%async_computation | async-start | bytes 2097152 | tf_op jit(solution)/shard_map/psum | solution.py:65
  43.6 236.5 %all-gather.6.cloned.1.call-start = ((), (), s32[]{:S(2)}) async-start(), calls=%async_computation.1 | async-start | bytes 2621440 | tf_op jit(solution)/shard_map/all_gather | solution.py:56
  44.4 311.9 %all-reduce.10.cloned.1.call-start = ((), (), s32[]{:S(2)}) async-start(), calls=%async_computation.2 | async-start | bytes 524288 | tf_op jit(solution)/shard_map/psum | solution.py:70
  44.8 217.1 %copy-start.1 = (f32[512,512]{1,0:T(8,128)}, f32[512,512]{1,0:T(8,128)S(1)}, u32[]{:S(2)}) copy-start(f32[512,512]{1,0:T(8,128)S(1)} %fusion.24) | copy-start | bytes 3145732
  265.5 24.9 %collective-permute-start = (f32[4,16,16,128]{3,2,1,0:T(8,128)S(1)}, f32[4,16,16,128]{3,2,1,0:T(8,128)S(1)}, u32[]{:S(2)}, u32[]{:S(2)}) collective-permute-start(f32[4,16,16,128]{3,2,1,0:T(8,128)S(1)} %bitcast.260), channel_id=1, source_target_pairs={{4,0},{8,4},{12,8},{16,12},{20,16},{24,20},{28,24},{0,28},{5,1},{9... | collective-permute-start | bytes 1572872 | tf_op jit(solution)/shard_map/ppermute | solution.py:23
  268.5 21.9 %collective-permute-start.1 = (f32[4,16,16,128]{3,2,1,0:T(8,128)S(1)}, f32[4,16,16,128]{3,2,1,0:T(8,128)S(1)}, u32[]{:S(2)}, u32[]{:S(2)}) collective-permute-start(f32[4,16,16,128]{3,2,1,0:T(8,128)S(1)} %bitcast.261), channel_id=1, source_target_pairs={{0,4},{4,8},{8,12},{12,16},{16,20},{20,24},{24,28},{28,0},{1,5},{5... | collective-permute-start | bytes 1572872 | tf_op jit(solution)/shard_map/ppermute | solution.py:20
  283.7 137.5 %all-gather.8.cloned.1.call-start = ((), (), s32[]{:S(2)}) async-start(), calls=%async_computation.3 | async-start | bytes 2621440 | tf_op jit(solution)/shard_map/all_gather | solution.py:63
  291.5 64.8 %copy-start = (f32[4,16,16,512]{3,2,1,0:T(8,128)S(1)}, f32[4,16,16,512]{3,2,1,0:T(8,128)}, u32[]{:S(2)}) copy-start(f32[4,16,16,512]{3,2,1,0:T(8,128)} %all-gather.6.cloned.1.call-done) | copy-start | bytes 6291460
  399.9 108.6 %all-reduce.12.cloned.1.call-start = ((), (), s32[]{:S(2)}) async-start(), calls=%async_computation.4 | async-start | bytes 2097152 | tf_op jit(solution)/shard_map/psum | solution.py:65
  430.1 327.3 %all-reduce.14.cloned.1.call-start = ((), (), s32[]{:S(2)}) async-start(), calls=%async_computation.5 | async-start | bytes 524288 | tf_op jit(solution)/shard_map/psum | solution.py:70
  563.3 96.4 %copy-start.2 = (f32[512,512]{1,0:T(8,128)S(1)}, f32[512,512]{1,0:T(8,128)}, u32[]{:S(2)}) copy-start(f32[512,512]{1,0:T(8,128)} %copy-done.1) | copy-start | bytes 3145732
  673.6 26.0 %collective-permute-start.2 = (f32[4,16,16,128]{3,2,1,0:T(8,128)S(1)}, f32[4,16,16,128]{3,2,1,0:T(8,128)}, u32[]{:S(2)}, u32[]{:S(2)}) collective-permute-start(f32[4,16,16,128]{3,2,1,0:T(8,128)S(1)} %bitcast.228), channel_id=1, source_target_pairs={{4,0},{8,4},{12,8},{16,12},{20,16},{24,20},{28,24},{0,28},{5,1},{9... | collective-permute-start | bytes 1572872 | tf_op jit(solution)/shard_map/ppermute | solution.py:23
  676.5 23.1 %collective-permute-start.3 = (f32[4,16,16,128]{3,2,1,0:T(8,128)S(1)}, f32[4,16,16,128]{3,2,1,0:T(8,128)}, u32[]{:S(2)}, u32[]{:S(2)}) collective-permute-start(f32[4,16,16,128]{3,2,1,0:T(8,128)S(1)} %bitcast.229), channel_id=1, source_target_pairs={{0,4},{4,8},{8,12},{12,16},{16,20},{20,24},{24,28},{28,0},{1,5},{5... | collective-permute-start | bytes 1572872 | tf_op jit(solution)/shard_map/ppermute | solution.py:20
  684.5 138.3 %all-gather.10.cloned.1.call-start = ((), (), s32[]{:S(2)}) async-start(), calls=%async_computation.6 | async-start | bytes 2621440 | tf_op jit(solution)/shard_map/all_gather | solution.py:63
  801.4 108.7 %all-reduce.16.cloned.1.call-start = ((), (), s32[]{:S(2)}) async-start(), calls=%async_computation.7 | async-start | bytes 2097152 | tf_op jit(solution)/shard_map/psum | solution.py:65
  831.6 327.6 %all-reduce.18.cloned.1.call-start = ((), (), s32[]{:S(2)}) async-start(), calls=%async_computation.8 | async-start | bytes 524288 | tf_op jit(solution)/shard_map/psum | solution.py:70
  964.9 96.6 %copy-start.3 = (f32[512,512]{1,0:T(8,128)S(1)}, f32[512,512]{1,0:T(8,128)}, u32[]{:S(2)}) copy-start(f32[512,512]{1,0:T(8,128)} %copy-done.1) | copy-start | bytes 3145732
  1075.4 26.0 %collective-permute-start.4 = (f32[4,16,16,128]{3,2,1,0:T(8,128)S(1)}, f32[4,16,16,128]{3,2,1,0:T(8,128)}, u32[]{:S(2)}, u32[]{:S(2)}) collective-permute-start(f32[4,16,16,128]{3,2,1,0:T(8,128)S(1)} %bitcast.247), channel_id=1, source_target_pairs={{4,0},{8,4},{12,8},{16,12},{20,16},{24,20},{28,24},{0,28},{5,1},{9... | collective-permute-start | bytes 1572872 | tf_op jit(solution)/shard_map/ppermute | solution.py:23
  1078.3 23.1 %collective-permute-start.5 = (f32[4,16,16,128]{3,2,1,0:T(8,128)S(1)}, f32[4,16,16,128]{3,2,1,0:T(8,128)}, u32[]{:S(2)}, u32[]{:S(2)}) collective-permute-start(f32[4,16,16,128]{3,2,1,0:T(8,128)S(1)} %bitcast.248), channel_id=1, source_target_pairs={{0,4},{4,8},{8,12},{12,16},{16,20},{20,24},{24,28},{28,0},{1,5},{5... | collective-permute-start | bytes 1572872 | tf_op jit(solution)/shard_map/ppermute | solution.py:20
  1086.4 15.0 %copy-start.24 = (f32[4,16,15,128]{3,2,1,0:T(8,128)S(1)}, f32[4,16,15,128]{3,2,1,0:T(8,128)}, u32[]{:S(2)}) copy-start(f32[4,16,15,128]{3,2,1,0:T(8,128)} %get-tuple-element.79) | copy-start | bytes 1474564
  1086.4 15.0 %copy-start.25 = (f32[4,16,15,128]{3,2,1,0:T(8,128)S(1)}, f32[4,16,15,128]{3,2,1,0:T(8,128)}, u32[]{:S(2)}) copy-start(f32[4,16,15,128]{3,2,1,0:T(8,128)} %get-tuple-element.80) | copy-start | bytes 1474564
  1086.4 15.0 %copy-start.26 = (f32[4,16,14,128]{3,2,1,0:T(8,128)S(1)}, f32[4,16,14,128]{3,2,1,0:T(8,128)}, u32[]{:S(2)}) copy-start(f32[4,16,14,128]{3,2,1,0:T(8,128)} %get-tuple-element.83) | copy-start | bytes 1376260
  1162.7 38.2 %copy-start.49 = (f32[1,128]{1,0:T(1,128)S(1)}, f32[1,128]{1,0:T(1,128)}, u32[]{:S(2)}) copy-start(f32[1,128]{1,0:T(1,128)} %get-tuple-element.189) | copy-start | bytes 1540
  (42 other events, 318.2 us)
Sparse Core Ops, SparseCore 0:
  9.5 25.2 all-gather.11
  43.8 78.2 all-reduce.7
  123.6 22.4 all-gather.5
  283.9 72.4 all-reduce.9
  400.0 21.2 all-gather.7
  430.2 78.2 all-reduce.11
  684.6 72.6 all-reduce.13
  801.5 21.2 all-gather.9
  831.7 78.2 all-reduce.15
  1086.5 72.6 all-reduce.17
